TPU v7x, 512 devices: a whole 4x8x8 slice. The times are simulated.
512 devices in a mesh: seq: 64 (over z_hi, x, y), head: 8 (over z_lo, core).
Axes of the slice: x: 4, y: 8, z: 8 (z_hi: 2, z_lo: 4; z = z_hi * 4 + z_lo), core: 2. Of those that a mesh axis runs over, the one named last changes fastest.
Arguments:
- queries: bfloat16 [12288, 32, 128], P('seq', 'head'), may hold values from -180 to 180
- key_rows: bfloat16 [12288, 8, 128], P('seq', 'head'), may hold values from -4.5 to 4.5
- value_rows: bfloat16 [12288, 8, 128], P('seq', 'head'), may hold values from -24 to 24
- windows: int32 [32], P('head'), may hold values from 768 to 1536, as said below
- sink_counts: int32 [32], P('head'), may hold values from 1 to 4, as said below
- sink_bias: float32 [32], P('head'), may hold values from 3 to 7
- out_weight: bfloat16 [4096, 4096], P('head'), may hold values from -0.09375 to 0.09375
Outputs:
- attn_out: bfloat16 [12288, 4096], P(('seq', 'head'))
Inputs may be any that keep to these rules, and one draw needn't show every extreme that they name: `windows`: each head's window lies between 768 and 1536, and some head has exactly 1536. `sink_counts`: each head has 1 to 4 sink tokens, and some head has exactly 4.
All inputs are finite; a program needn't handle non-finite values.
Results may differ from a plain program's by a relative error of at most 0.018.
Values may be sent and summed in bfloat16 or wider, within the bound.
A program may use at most 64 MiB of HBM per device.

v0:
```python
import jax
import jax.numpy as jnp
from jax import lax
from jax.sharding import Mesh
from jax.sharding import PartitionSpec as P

WINDOW = 1536
SINKS = 4
SEQ = ("seq_0", "seq_1", "seq_2")
SEQ_HEAD = ("seq_0", "seq_1", "seq_2", "head")


def shifted(block, axis, distance):
    devices = range(lax.axis_size(axis))
    route = [(i - distance, i) for i in devices if i - distance in devices]
    return lax.ppermute(block, axis, route)


def broadcast_by_axis(shard, axes, root):
    shard = jnp.where(lax.axis_index(axes) == root, shard, jnp.zeros_like(shard))
    for axis in axes:
        shard = lax.psum(shard, axis)
    return shard


def cut_along(shard, dim, length):
    dims = shard.shape
    blocks = shard.reshape(*dims[:dim], length, dims[dim] // length, *dims[dim + 1 :])
    return jnp.moveaxis(blocks, dim, 0)


def sent_and_summed(shard, axis, dim):
    blocks = cut_along(shard, dim, lax.axis_size(axis))
    arrived = lax.all_to_all(blocks, axis, split_axis=0, concat_axis=0, tiled=True)
    return arrived.astype(jnp.float32).sum(axis=0)


def attend_block(query_block, band_rows, sink_rows, first_pos, windows, sink_counts, sink_bias):
    tok_rows, local_heads, head_width = query_block.shape
    kv_local = band_rows.shape[2]
    group_size = local_heads // kv_local
    band_span = band_rows.shape[1]
    sink_total = sink_rows.shape[1]
    all_keys = jnp.concatenate([sink_rows[0], band_rows[0]], axis=0)
    all_values = jnp.concatenate([sink_rows[1], band_rows[1]], axis=0)
    grouped = query_block.reshape(tok_rows, kv_local, group_size, head_width)
    score_scale = 1.0 / head_width**0.5
    scores = (
        jnp.einsum("tkgd,skd->kgts", grouped, all_keys, preferred_element_type=jnp.float32)
        * score_scale
    )
    query_pos = first_pos + jnp.arange(tok_rows, dtype=jnp.int32)
    band_pos = first_pos + tok_rows - band_span + jnp.arange(band_span, dtype=jnp.int32)
    sink_pos = jnp.arange(sink_total, dtype=jnp.int32)
    key_pos = jnp.concatenate([sink_pos, band_pos])
    is_sink = jnp.concatenate([jnp.ones((sink_total,), bool), jnp.zeros((band_span,), bool)])
    head_window = windows.reshape(kv_local, group_size, 1, 1)
    head_sinks = sink_counts.reshape(kv_local, group_size, 1, 1)
    head_bias = sink_bias.reshape(kv_local, group_size, 1, 1)
    distance = query_pos[:, None] - key_pos[None, :]
    visible = (distance >= 0) & jnp.where(
        is_sink, key_pos < head_sinks, (distance < head_window) & (key_pos >= head_sinks)
    )
    scores = scores + jnp.where(is_sink, head_bias, 0.0)
    masked = jnp.where(visible, scores, -1e30)
    highest = jnp.max(masked, axis=-1, keepdims=True)
    weights = jnp.where(visible, jnp.exp(masked - highest), 0.0)
    normed = (weights / jnp.sum(weights, axis=-1, keepdims=True)).astype(jnp.bfloat16)
    mixed = jnp.einsum("kgts,skd->tkgd", normed, all_values, preferred_element_type=jnp.float32)
    return mixed.astype(jnp.bfloat16).reshape(tok_rows, local_heads * head_width)


def shards(queries, key_rows, value_rows, windows, sink_counts, sink_bias, out_weight):
    tok_rows = queries.shape[0]
    stacked = jnp.stack([key_rows, value_rows])
    halo_depth = (WINDOW - 1) // tok_rows + 1
    received = [shifted(stacked, SEQ, halo_depth - number) for number in range(halo_depth)]
    halo_rows = jnp.concatenate(received, axis=1)
    band_all = jnp.concatenate([halo_rows, stacked], axis=1)
    sink_rows = broadcast_by_axis(stacked[:, :SINKS], SEQ, 0)
    first_pos = lax.axis_index(SEQ) * tok_rows
    attended = attend_block(
        queries, band_all, sink_rows, first_pos, windows, sink_counts, sink_bias
    )
    mine = sent_and_summed(
        jnp.dot(attended, out_weight, preferred_element_type=jnp.float32).astype(jnp.bfloat16),
        "head",
        0,
    )
    return mine.astype(jnp.bfloat16)


def solution(mesh):
    split = Mesh(
        mesh.devices.reshape(2, 4, 8, mesh.shape["head"]), ("seq_0", "seq_1", "seq_2", "head")
    )
    return jax.shard_map(
        shards,
        mesh=split,
        in_specs=(
            P(SEQ, "head", None),
            P(SEQ, "head", None),
            P(SEQ, "head", None),
            P("head"),
            P("head"),
            P("head"),
            P("head", None),
        ),
        out_specs=P(SEQ_HEAD, None),
        check_vma=False,
    )
```

profile of v0, /device:TPU:256, one launch (start us, length us, event | category | flops | bytes accessed | tf_op | source)
XLA Modules:
  0.0 160.0 jit_solution(8025812477693680216)
XLA Ops:
  0.0 0.0 copy-start
  0.0 0.0 copy-start.2
  0.0 0.0 copy-start.3
  0.0 0.9 pad_maximum_fusion
  0.9 4.5 %collective-permute-start.6 = (bf16[2,192,1,128]{3,1,2,0:T(8,128)(2,1)S(1)}, bf16[2,192,1,128]{3,1,2,0:T(8,128)(2,1)S(1)}, u32[]{:S(2)}, u32[]{:S(2)}) collective-permute-start(bf16[2,192,1,128]{3,1,2,0:T(8,128)(2,1)S(1)} %pad_maximum_fusion), channel_id=1, source_target_pairs={{0,16},{8,24},{16,32},{24,40},{32,48},{40,56},{48,64},{56,72},{64,... | collective-permute-start | bytes 294920 | tf_op jit(solution)/shard_map/ppermute | solution.py:16
  5.4 5.8 %collective-permute-start.5 = (bf16[2,192,1,128]{3,1,2,0:T(8,128)(2,1)S(1)}, bf16[2,192,1,128]{3,1,2,0:T(8,128)(2,1)S(1)}, u32[]{:S(2)}, u32[]{:S(2)}) collective-permute-start(bf16[2,192,1,128]{3,1,2,0:T(8,128)(2,1)S(1)} %pad_maximum_fusion), channel_id=1, source_target_pairs={{0,24},{8,32},{16,40},{24,48},{32,56},{40,64},{48,72},{56,80},{64,... | collective-permute-start | bytes 294920 | tf_op jit(solution)/shard_map/ppermute | solution.py:16
  11.2 3.8 %collective-permute-start.4 = (bf16[2,192,1,128]{3,1,2,0:T(8,128)(2,1)S(1)}, bf16[2,192,1,128]{3,1,2,0:T(8,128)(2,1)S(1)}, u32[]{:S(2)}, u32[]{:S(2)}) collective-permute-start(bf16[2,192,1,128]{3,1,2,0:T(8,128)(2,1)S(1)} %pad_maximum_fusion), channel_id=1, source_target_pairs={{0,32},{8,40},{16,48},{24,56},{32,64},{40,72},{48,80},{56,88},{64,... | collective-permute-start | bytes 294920 | tf_op jit(solution)/shard_map/ppermute | solution.py:16
  15.1 6.0 %collective-permute-start.3 = (bf16[2,192,1,128]{3,1,2,0:T(8,128)(2,1)S(1)}, bf16[2,192,1,128]{3,1,2,0:T(8,128)(2,1)S(1)}, u32[]{:S(2)}, u32[]{:S(2)}) collective-permute-start(bf16[2,192,1,128]{3,1,2,0:T(8,128)(2,1)S(1)} %pad_maximum_fusion), channel_id=1, source_target_pairs={{0,40},{8,48},{16,56},{24,64},{32,72},{40,80},{48,88},{56,96},{64,... | collective-permute-start | bytes 294920 | tf_op jit(solution)/shard_map/ppermute | solution.py:16
  21.1 3.4 %collective-permute-start = (bf16[2,192,1,128]{3,1,2,0:T(8,128)(2,1)S(1)}, bf16[2,192,1,128]{3,1,2,0:T(8,128)(2,1)S(1)}, u32[]{:S(2)}, u32[]{:S(2)}) collective-permute-start(bf16[2,192,1,128]{3,1,2,0:T(8,128)(2,1)S(1)} %pad_maximum_fusion), channel_id=1, source_target_pairs={{0,64},{8,72},{16,80},{24,88},{32,96},{40,104},{48,112},{56,120},{... | collective-permute-start | bytes 294920 | tf_op jit(solution)/shard_map/ppermute | solution.py:16
  24.6 0.1 pad_add_fusion
  24.7 0.3 broadcast_compare_fusion
  25.0 0.2 broadcast_subtract_fusion
  25.1 0.7 fusion.20
  25.8 8.8 %psum.21 = bf16[2,4,1,128]{3,1,2,0:T(4,128)(2,1)S(1)} all-reduce(bf16[2,4,1,128]{3,1,2,0:T(4,128)(2,1)S(1)} %fusion.20), channel_id=1, replica_groups=mesh['seq_0'=2,'seq_1'=4,'seq_2'=8,'head'=8] {'seq_0'}, use_global_device_ids=true, to_apply=%region_0.1 | all-reduce | flops 1024 | bytes 4096 | tf_op jit(solution)/shard_map/psum | solution.py:22
  34.7 9.5 %psum.22 = bf16[2,4,1,128]{3,1,2,0:T(4,128)(2,1)S(1)} all-reduce(bf16[2,4,1,128]{3,1,2,0:T(4,128)(2,1)S(1)} %psum.21), channel_id=1, replica_groups=mesh['seq_0'=2,'seq_1'=4,'seq_2'=8,'head'=8] {'seq_1'}, use_global_device_ids=true, to_apply=%region_1.2 | all-reduce | flops 1024 | bytes 4096 | tf_op jit(solution)/shard_map/psum | solution.py:22
  44.1 16.7 %psum.23 = bf16[2,4,1,128]{3,1,2,0:T(4,128)(2,1)S(1)} all-reduce(bf16[2,4,1,128]{3,1,2,0:T(4,128)(2,1)S(1)} %psum.22), channel_id=1, replica_groups=mesh['seq_0'=2,'seq_1'=4,'seq_2'=8,'head'=8] {'seq_2'}, use_global_device_ids=true, to_apply=%region_2.3 | all-reduce | flops 1024 | bytes 4096 | tf_op jit(solution)/shard_map/psum | solution.py:22
  60.8 0.7 broadcast_compare_fusion.2
  61.6 0.8 broadcast_select_fusion
  62.4 0.0 collective-permute-done
  62.4 3.9 %collective-permute-start.1 = (bf16[2,192,1,128]{3,1,2,0:T(8,128)(2,1)S(1)}, bf16[2,192,1,128]{3,1,2,0:T(8,128)(2,1)S(1)}, u32[]{:S(2)}, u32[]{:S(2)}) collective-permute-start(bf16[2,192,1,128]{3,1,2,0:T(8,128)(2,1)S(1)} %pad_maximum_fusion), channel_id=1, source_target_pairs={{0,56},{8,64},{16,72},{24,80},{32,88},{40,96},{48,104},{56,112},{6... | collective-permute-start | bytes 294920 | tf_op jit(solution)/shard_map/ppermute | solution.py:16
  66.3 9.5 %collective-permute-done.1 = bf16[2,192,1,128]{3,1,2,0:T(8,128)(2,1)S(1)} collective-permute-done((bf16[2,192,1,128]{3,1,2,0:T(8,128)(2,1)S(1)}, bf16[2,192,1,128]{3,1,2,0:T(8,128)(2,1)S(1)}, u32[]{:S(2)}, u32[]{:S(2)}) %collective-permute-start.1) | collective-permute-done | bytes 98336 | tf_op jit(solution)/shard_map/ppermute | solution.py:16
  75.8 3.3 %collective-permute-start.2 = (bf16[2,192,1,128]{3,1,2,0:T(8,128)(2,1)S(1)}, bf16[2,192,1,128]{3,1,2,0:T(8,128)(2,1)S(1)}, u32[]{:S(2)}, u32[]{:S(2)}) collective-permute-start(bf16[2,192,1,128]{3,1,2,0:T(8,128)(2,1)S(1)} %pad_maximum_fusion), channel_id=1, source_target_pairs={{0,48},{8,56},{16,64},{24,72},{32,80},{40,88},{48,96},{56,104},{64... | collective-permute-start | bytes 294920 | tf_op jit(solution)/shard_map/ppermute | solution.py:16
  79.2 10.9 %collective-permute-done.2 = bf16[2,192,1,128]{3,1,2,0:T(8,128)(2,1)S(1)} collective-permute-done((bf16[2,192,1,128]{3,1,2,0:T(8,128)(2,1)S(1)}, bf16[2,192,1,128]{3,1,2,0:T(8,128)(2,1)S(1)}, u32[]{:S(2)}, u32[]{:S(2)}) %collective-permute-start.2) | collective-permute-done | bytes 98336 | tf_op jit(solution)/shard_map/ppermute | solution.py:16
  90.1 5.0 %collective-permute-start.7 = (bf16[2,192,1,128]{3,1,2,0:T(8,128)(2,1)S(1)}, bf16[2,192,1,128]{3,1,2,0:T(8,128)(2,1)S(1)}, u32[]{:S(2)}, u32[]{:S(2)}) collective-permute-start(bf16[2,192,1,128]{3,1,2,0:T(8,128)(2,1)S(1)} %pad_maximum_fusion), channel_id=1, source_target_pairs={{0,8},{8,16},{16,24},{24,32},{32,40},{40,48},{48,56},{56,64},{64,7... | collective-permute-start | bytes 294920 | tf_op jit(solution)/shard_map/ppermute | solution.py:16
  95.1 0.0 collective-permute-done.3
  95.1 0.0 collective-permute-done.4
  95.2 0.0 collective-permute-done.5
  95.2 0.0 collective-permute-done.6
  95.2 9.5 %collective-permute-done.7 = bf16[2,192,1,128]{3,1,2,0:T(8,128)(2,1)S(1)} collective-permute-done((bf16[2,192,1,128]{3,1,2,0:T(8,128)(2,1)S(1)}, bf16[2,192,1,128]{3,1,2,0:T(8,128)(2,1)S(1)}, u32[]{:S(2)}, u32[]{:S(2)}) %collective-permute-start.7) | collective-permute-done | bytes 98336 | tf_op jit(solution)/shard_map/ppermute | solution.py:16
  104.7 0.8 constant_dynamic-update-slice_fusion
  105.6 0.1 slice_bitcast_fusion.1
  105.6 0.0 copy-done
  105.7 0.0 copy-done.2
  105.7 0.0 copy-done.3
  105.7 2.3 %fusion.1 = (f32[4,192]{1,0:T(4,128)S(1)}, f32[1732,192,4]{0,1,2:T(8,128)S(1)}) fusion(f32[4,1732]{1,0:T(4,128)S(1)} %broadcast_select_fusion, s32[192,1732]{1,0:T(8,128)S(1)} %broadcast_subtract_fusion, s32[4]{0:T(128)S(1)} %copy-done.3, pred[4,1732]{1,0:T(4,128)(4,1)S(1)} %get-tuple-element.8, pred[4,1732]{1,0:T(4,128)(4,1)S(1)} %get-tuple-element.7, ...), kind=kOutput, calls=%fused_computation.6 | convolution fusion | flops 352052480 | bytes 7669812 | tf_op jit(solution)/shard_map/tkgd,skd->kgts/dot_general | solution.py:49
  108.0 3.5 %fusion.4 = f32[4,192]{1,0:T(4,128)S(1)} fusion(f32[4,192]{1,0:T(4,128)S(1)} %get-tuple-element.11, f32[4,1732]{1,0:T(4,128)S(1)} %broadcast_select_fusion, f32[1732,192,4]{0,1,2:T(8,128)S(1)} %get-tuple-element.12, pred[4,1732]{1,0:T(4,128)(4,1)S(1)} %get-tuple-element.8, s32[4]{0:T(128)S(1)} %copy-done.3, s32[192,1732]{1,0:T(8,128)S(1)} %broadcast_subtract_fusion, ...), kind=kLoop, calls=%fused_computation.9 | loop fusion | flops 13300992 | bytes 7032884 | tf_op jit(solution)/shard_map/reduce_sum | solution.py:68
  111.5 0.0 copy-start.1
  111.5 2.8 %fusion.8 = bf16[192,1,4,128]{3,0,2,1:T(8,128)(2,1)S(1)} fusion(f32[4,192]{1,0:T(4,128)S(1)} %fusion.4, f32[4,192]{1,0:T(4,128)S(1)} %get-tuple-element.11, f32[4,1732]{1,0:T(4,128)S(1)} %broadcast_select_fusion, f32[1732,192,4]{0,1,2:T(8,128)S(1)} %get-tuple-element.12, pred[4,1732]{1,0:T(4,128)(4,1)S(1)} %get-tuple-element.8, s32[4]{0:T(128)S(1)} %copy-done.3, ...), kind=kOutput, calls=%fused_computation.11 | convolution fusion | flops 356142080 | bytes 7672884 | tf_op jit(solution)/shard_map/kgts,skd->tkgd/dot_general | solution.py:69
  114.4 0.2 copy.10
  114.5 0.0 copy-done.1
  114.5 1.0 convolution_convert_fusion
  115.5 43.5 %all_to_all.5 = bf16[8,24,4096]{2,1,0:T(8,128)(2,1)S(1)} all-to-all(bf16[8,24,4096]{2,1,0:T(8,128)(2,1)S(1)} %bitcast.58), channel_id=1, replica_groups=mesh['seq_0'=2,'seq_1'=4,'seq_2'=8,'head'=8] {'head'}, dimensions={0} | all-to-all | bytes 3145728 | tf_op jit(solution)/shard_map/all_to_all | solution.py:34
  159.1 0.9 reduce_sum.22
  (12 shorter events, 0.1 us)
Async XLA Ops:
  0.0 105.7 %copy-start = (bf16[192,4,128]{2,1,0:T(4,128)(2,1)S(1)}, bf16[192,4,128]{2,1,0:T(4,128)(2,1)}, u32[]{:S(2)}) copy-start(bf16[192,4,128]{2,1,0:T(4,128)(2,1)} %param.7) | copy-start | bytes 589828
  0.0 105.7 %copy-start.2 = (pred[1732]{0:T(1024)(128)(4,1)S(1)}, pred[1732]{0:T(1024)(128)(4,1)}, u32[]{:S(2)}) copy-start(pred[1732]{0:T(1024)(128)(4,1)} %constant.37.clone.1) | copy-start | bytes 5200
  0.0 105.7 %copy-start.3 = (s32[4]{0:T(128)S(1)}, s32[4]{0:T(128)}, u32[]{:S(2)}) copy-start(s32[4]{0:T(128)} %param.10) | copy-start | bytes 52
  0.9 94.3 %collective-permute-start.6 = (bf16[2,192,1,128]{3,1,2,0:T(8,128)(2,1)S(1)}, bf16[2,192,1,128]{3,1,2,0:T(8,128)(2,1)S(1)}, u32[]{:S(2)}, u32[]{:S(2)}) collective-permute-start(bf16[2,192,1,128]{3,1,2,0:T(8,128)(2,1)S(1)} %pad_maximum_fusion), channel_id=1, source_target_pairs={{0,16},{8,24},{16,32},{24,40},{32,48},{40,56},{48,64},{56,72},{64,... | collective-permute-start | bytes 294920 | tf_op jit(solution)/shard_map/ppermute | solution.py:16
  5.4 89.8 %collective-permute-start.5 = (bf16[2,192,1,128]{3,1,2,0:T(8,128)(2,1)S(1)}, bf16[2,192,1,128]{3,1,2,0:T(8,128)(2,1)S(1)}, u32[]{:S(2)}, u32[]{:S(2)}) collective-permute-start(bf16[2,192,1,128]{3,1,2,0:T(8,128)(2,1)S(1)} %pad_maximum_fusion), channel_id=1, source_target_pairs={{0,24},{8,32},{16,40},{24,48},{32,56},{40,64},{48,72},{56,80},{64,... | collective-permute-start | bytes 294920 | tf_op jit(solution)/shard_map/ppermute | solution.py:16
  11.2 83.9 %collective-permute-start.4 = (bf16[2,192,1,128]{3,1,2,0:T(8,128)(2,1)S(1)}, bf16[2,192,1,128]{3,1,2,0:T(8,128)(2,1)S(1)}, u32[]{:S(2)}, u32[]{:S(2)}) collective-permute-start(bf16[2,192,1,128]{3,1,2,0:T(8,128)(2,1)S(1)} %pad_maximum_fusion), channel_id=1, source_target_pairs={{0,32},{8,40},{16,48},{24,56},{32,64},{40,72},{48,80},{56,88},{64,... | collective-permute-start | bytes 294920 | tf_op jit(solution)/shard_map/ppermute | solution.py:16
  15.1 80.0 %collective-permute-start.3 = (bf16[2,192,1,128]{3,1,2,0:T(8,128)(2,1)S(1)}, bf16[2,192,1,128]{3,1,2,0:T(8,128)(2,1)S(1)}, u32[]{:S(2)}, u32[]{:S(2)}) collective-permute-start(bf16[2,192,1,128]{3,1,2,0:T(8,128)(2,1)S(1)} %pad_maximum_fusion), channel_id=1, source_target_pairs={{0,40},{8,48},{16,56},{24,64},{32,72},{40,80},{48,88},{56,96},{64,... | collective-permute-start | bytes 294920 | tf_op jit(solution)/shard_map/ppermute | solution.py:16
  21.1 41.2 %collective-permute-start = (bf16[2,192,1,128]{3,1,2,0:T(8,128)(2,1)S(1)}, bf16[2,192,1,128]{3,1,2,0:T(8,128)(2,1)S(1)}, u32[]{:S(2)}, u32[]{:S(2)}) collective-permute-start(bf16[2,192,1,128]{3,1,2,0:T(8,128)(2,1)S(1)} %pad_maximum_fusion), channel_id=1, source_target_pairs={{0,64},{8,72},{16,80},{24,88},{32,96},{40,104},{48,112},{56,120},{... | collective-permute-start | bytes 294920 | tf_op jit(solution)/shard_map/ppermute | solution.py:16
  62.4 13.4 %collective-permute-start.1 = (bf16[2,192,1,128]{3,1,2,0:T(8,128)(2,1)S(1)}, bf16[2,192,1,128]{3,1,2,0:T(8,128)(2,1)S(1)}, u32[]{:S(2)}, u32[]{:S(2)}) collective-permute-start(bf16[2,192,1,128]{3,1,2,0:T(8,128)(2,1)S(1)} %pad_maximum_fusion), channel_id=1, source_target_pairs={{0,56},{8,64},{16,72},{24,80},{32,88},{40,96},{48,104},{56,112},{6... | collective-permute-start | bytes 294920 | tf_op jit(solution)/shard_map/ppermute | solution.py:16
  75.8 14.3 %collective-permute-start.2 = (bf16[2,192,1,128]{3,1,2,0:T(8,128)(2,1)S(1)}, bf16[2,192,1,128]{3,1,2,0:T(8,128)(2,1)S(1)}, u32[]{:S(2)}, u32[]{:S(2)}) collective-permute-start(bf16[2,192,1,128]{3,1,2,0:T(8,128)(2,1)S(1)} %pad_maximum_fusion), channel_id=1, source_target_pairs={{0,48},{8,56},{16,64},{24,72},{32,80},{40,88},{48,96},{56,104},{64... | collective-permute-start | bytes 294920 | tf_op jit(solution)/shard_map/ppermute | solution.py:16
  90.1 14.6 %collective-permute-start.7 = (bf16[2,192,1,128]{3,1,2,0:T(8,128)(2,1)S(1)}, bf16[2,192,1,128]{3,1,2,0:T(8,128)(2,1)S(1)}, u32[]{:S(2)}, u32[]{:S(2)}) collective-permute-start(bf16[2,192,1,128]{3,1,2,0:T(8,128)(2,1)S(1)} %pad_maximum_fusion), channel_id=1, source_target_pairs={{0,8},{8,16},{16,24},{24,32},{32,40},{40,48},{48,56},{56,64},{64,7... | collective-permute-start | bytes 294920 | tf_op jit(solution)/shard_map/ppermute | solution.py:16
  111.5 3.0 %copy-start.1 = (bf16[512,4096]{1,0:T(8,128)(2,1)S(1)}, bf16[512,4096]{1,0:T(8,128)(2,1)}, u32[]{:S(2)}) copy-start(bf16[512,4096]{1,0:T(8,128)(2,1)} %param.13) | copy-start | bytes 12582916
where the time goes:
time: 161 us; the launch traced here: 160 us
  blocking collectives  78.5 us (49%)
  starting transfers between devices  35.8 us (22%)
  waiting for transfers between devices  29.9 us (19%)
  other arithmetic  8.87 us (6%)
  matrix products  6.17 us (4%)
    all_to_all x1, blocking collectives, sent_and_summed(): lax.all_to_all(blocks, axis, split_axis=0, concat_axis=0, tiled=True)  43.5 us
    ppermute x8, starting transfers between devices, shifted(): return lax.ppermute(block, axis, route)  35.8 us
    psum x3, blocking collectives, broadcast_by_axis(): shard = lax.psum(shard, axis)  35 us
    ppermute x8, waiting for transfers between devices, shifted(): return lax.ppermute(block, axis, route)  29.9 us
    reduce_sum x1, other arithmetic, attend_block(): jnp.sum(weights, axis=-1, keepdims=True)  3.48 us
  transfers between devices with their start and end apart: 8, of which 3 were waited for; matrix products, arithmetic and copies ran while one was open for 2% of the time, Pallas kernels for 0%

commit v1 on v0

--- a/solution.py
+++ b/solution.py
@@ -19,7 +19,11 @@
 def broadcast_by_axis(shard, axes, root):
     shard = jnp.where(lax.axis_index(axes) == root, shard, jnp.zeros_like(shard))
     for axis in axes:
-        shard = lax.psum(shard, axis)
+
+        def get_arrays_here(local_array):
+            return lax.all_gather(local_array, axis_name=axis).sum(axis=0)
+
+        shard = get_arrays_here(shard)
     return shard
 
 

time: 161 us -> 169 us (1.050)
  blocking collectives: 78.5 us -> 86.2 us
  waiting for transfers between devices: 29.9 us -> 35.8 us
  starting transfers between devices: 35.8 us -> 30.5 us
    all_gather x0 -> x3, blocking collectives: none -> 42.7 us  [get_arrays_here(): return lax.all_gather(local_array, axis_name=axis).sum(axis=0)]
    psum x3 -> x0, blocking collectives: 35 us -> none  [broadcast_by_axis(): shard = lax.psum(shard, axis)]
    ppermute x8, waiting for transfers between devices: 29.9 us -> 35.8 us  [shifted(): return lax.ppermute(block, axis, route)]
    ppermute x8, starting transfers between devices: 35.8 us -> 30.5 us  [shifted(): return lax.ppermute(block, axis, route)]
where the time goes in v1:
time: 169 us; the launch traced here: 168 us
  blocking collectives  86.2 us (51%)
  waiting for transfers between devices  35.8 us (21%)
  starting transfers between devices  30.5 us (18%)
  other arithmetic  8.92 us (5%)
  matrix products  6.18 us (4%)
    all_to_all x1, blocking collectives, sent_and_summed(): lax.all_to_all(blocks, axis, split_axis=0, concat_axis=0, tiled=True)  43.5 us
    all_gather x3, blocking collectives, get_arrays_here(): return lax.all_gather(local_array, axis_name=axis).sum(axis=0)  42.7 us
    ppermute x8, waiting for transfers between devices, shifted(): return lax.ppermute(block, axis, route)  35.8 us
    ppermute x8, starting transfers between devices, shifted(): return lax.ppermute(block, axis, route)  30.5 us
    reduce_sum x1, other arithmetic, attend_block(): jnp.sum(weights, axis=-1, keepdims=True)  3.48 us
  transfers between devices with their start and end apart: 8, of which 3 were waited for; matrix products, arithmetic and copies ran while one was open for 2% of the time, Pallas kernels for 0%

profile of v1, /device:TPU:256, one launch (start us, length us, event | category | flops | bytes accessed | tf_op | source)
XLA Modules:
  0.0 168.2 jit_solution(15527921884242209961)
XLA Ops:
  0.0 0.0 copy-start
  0.0 0.0 copy-start.2
  0.0 0.0 copy-start.3
  0.0 0.9 pad_maximum_fusion
  0.9 4.5 %collective-permute-start.6 = (bf16[2,192,1,128]{3,1,2,0:T(8,128)(2,1)S(1)}, bf16[2,192,1,128]{3,1,2,0:T(8,128)(2,1)S(1)}, u32[]{:S(2)}, u32[]{:S(2)}) collective-permute-start(bf16[2,192,1,128]{3,1,2,0:T(8,128)(2,1)S(1)} %pad_maximum_fusion), channel_id=1, source_target_pairs={{0,16},{8,24},{16,32},{24,40},{32,48},{40,56},{48,64},{56,72},{64,... | collective-permute-start | bytes 294920 | tf_op jit(solution)/shard_map/ppermute | solution.py:16
  5.4 5.8 %collective-permute-start.5 = (bf16[2,192,1,128]{3,1,2,0:T(8,128)(2,1)S(1)}, bf16[2,192,1,128]{3,1,2,0:T(8,128)(2,1)S(1)}, u32[]{:S(2)}, u32[]{:S(2)}) collective-permute-start(bf16[2,192,1,128]{3,1,2,0:T(8,128)(2,1)S(1)} %pad_maximum_fusion), channel_id=1, source_target_pairs={{0,24},{8,32},{16,40},{24,48},{32,56},{40,64},{48,72},{56,80},{64,... | collective-permute-start | bytes 294920 | tf_op jit(solution)/shard_map/ppermute | solution.py:16
  11.2 3.8 %collective-permute-start.4 = (bf16[2,192,1,128]{3,1,2,0:T(8,128)(2,1)S(1)}, bf16[2,192,1,128]{3,1,2,0:T(8,128)(2,1)S(1)}, u32[]{:S(2)}, u32[]{:S(2)}) collective-permute-start(bf16[2,192,1,128]{3,1,2,0:T(8,128)(2,1)S(1)} %pad_maximum_fusion), channel_id=1, source_target_pairs={{0,32},{8,40},{16,48},{24,56},{32,64},{40,72},{48,80},{56,88},{64,... | collective-permute-start | bytes 294920 | tf_op jit(solution)/shard_map/ppermute | solution.py:16
  15.1 6.0 %collective-permute-start.3 = (bf16[2,192,1,128]{3,1,2,0:T(8,128)(2,1)S(1)}, bf16[2,192,1,128]{3,1,2,0:T(8,128)(2,1)S(1)}, u32[]{:S(2)}, u32[]{:S(2)}) collective-permute-start(bf16[2,192,1,128]{3,1,2,0:T(8,128)(2,1)S(1)} %pad_maximum_fusion), channel_id=1, source_target_pairs={{0,40},{8,48},{16,56},{24,64},{32,72},{40,80},{48,88},{56,96},{64,... | collective-permute-start | bytes 294920 | tf_op jit(solution)/shard_map/ppermute | solution.py:16
  21.1 3.4 %collective-permute-start = (bf16[2,192,1,128]{3,1,2,0:T(8,128)(2,1)S(1)}, bf16[2,192,1,128]{3,1,2,0:T(8,128)(2,1)S(1)}, u32[]{:S(2)}, u32[]{:S(2)}) collective-permute-start(bf16[2,192,1,128]{3,1,2,0:T(8,128)(2,1)S(1)} %pad_maximum_fusion), channel_id=1, source_target_pairs={{0,64},{8,72},{16,80},{24,88},{32,96},{40,104},{48,112},{56,120},{... | collective-permute-start | bytes 294920 | tf_op jit(solution)/shard_map/ppermute | solution.py:16
  24.6 0.1 pad_add_fusion
  24.7 0.3 broadcast_compare_fusion
  25.0 0.2 broadcast_subtract_fusion
  25.1 0.7 fusion.20
  25.8 8.3 %all-gather = bf16[4,4,1,128]{3,1,2,0:T(4,128)(2,1)S(1)} all-gather(bf16[2,4,1,128]{3,1,2,0:T(4,128)(2,1)S(1)} %fusion.20), channel_id=2, replica_groups=mesh['seq_0'=2,'seq_1'=4,'seq_2'=8,'head'=8] {'seq_0'}, dimensions={0}, use_global_device_ids=true | all-gather | bytes 6144 | tf_op jit(solution)/shard_map/all_gather | solution.py:24
  34.1 10.4 %all-gather.1 = bf16[8,4,128]{2,1,0:T(4,128)(2,1)S(1)} all-gather(bf16[2,4,128]{2,1,0:T(4,128)(2,1)S(1)} %reduce.9), channel_id=3, replica_groups=mesh['seq_0'=2,'seq_1'=4,'seq_2'=8,'head'=8] {'seq_1'}, dimensions={0}, use_global_device_ids=true | all-gather | bytes 10240 | tf_op jit(solution)/shard_map/all_gather | solution.py:24
  44.6 24.0 %all-gather.2 = bf16[16,4,128]{2,1,0:T(4,128)(2,1)S(1)} all-gather(bf16[2,4,128]{2,1,0:T(4,128)(2,1)S(1)} %reduce.10), channel_id=4, replica_groups=mesh['seq_0'=2,'seq_1'=4,'seq_2'=8,'head'=8] {'seq_2'}, dimensions={0}, use_global_device_ids=true | all-gather | bytes 18432 | tf_op jit(solution)/shard_map/all_gather | solution.py:24
  68.5 0.7 broadcast_compare_fusion.2
  69.3 0.8 broadcast_select_fusion
  70.1 0.0 collective-permute-done
  70.1 1.9 %collective-permute-start.1 = (bf16[2,192,1,128]{3,1,2,0:T(8,128)(2,1)S(1)}, bf16[2,192,1,128]{3,1,2,0:T(8,128)(2,1)S(1)}, u32[]{:S(2)}, u32[]{:S(2)}) collective-permute-start(bf16[2,192,1,128]{3,1,2,0:T(8,128)(2,1)S(1)} %pad_maximum_fusion), channel_id=1, source_target_pairs={{0,56},{8,64},{16,72},{24,80},{32,88},{40,96},{48,104},{56,112},{6... | collective-permute-start | bytes 294920 | tf_op jit(solution)/shard_map/ppermute | solution.py:16
  72.0 11.5 %collective-permute-done.1 = bf16[2,192,1,128]{3,1,2,0:T(8,128)(2,1)S(1)} collective-permute-done((bf16[2,192,1,128]{3,1,2,0:T(8,128)(2,1)S(1)}, bf16[2,192,1,128]{3,1,2,0:T(8,128)(2,1)S(1)}, u32[]{:S(2)}, u32[]{:S(2)}) %collective-permute-start.1) | collective-permute-done | bytes 98336 | tf_op jit(solution)/shard_map/ppermute | solution.py:16
  83.5 3.1 %collective-permute-start.2 = (bf16[2,192,1,128]{3,1,2,0:T(8,128)(2,1)S(1)}, bf16[2,192,1,128]{3,1,2,0:T(8,128)(2,1)S(1)}, u32[]{:S(2)}, u32[]{:S(2)}) collective-permute-start(bf16[2,192,1,128]{3,1,2,0:T(8,128)(2,1)S(1)} %pad_maximum_fusion), channel_id=1, source_target_pairs={{0,48},{8,56},{16,64},{24,72},{32,80},{40,88},{48,96},{56,104},{64... | collective-permute-start | bytes 294920 | tf_op jit(solution)/shard_map/ppermute | solution.py:16
  86.6 11.7 %collective-permute-done.2 = bf16[2,192,1,128]{3,1,2,0:T(8,128)(2,1)S(1)} collective-permute-done((bf16[2,192,1,128]{3,1,2,0:T(8,128)(2,1)S(1)}, bf16[2,192,1,128]{3,1,2,0:T(8,128)(2,1)S(1)}, u32[]{:S(2)}, u32[]{:S(2)}) %collective-permute-start.2) | collective-permute-done | bytes 98336 | tf_op jit(solution)/shard_map/ppermute | solution.py:16
  98.3 1.9 %collective-permute-start.7 = (bf16[2,192,1,128]{3,1,2,0:T(8,128)(2,1)S(1)}, bf16[2,192,1,128]{3,1,2,0:T(8,128)(2,1)S(1)}, u32[]{:S(2)}, u32[]{:S(2)}) collective-permute-start(bf16[2,192,1,128]{3,1,2,0:T(8,128)(2,1)S(1)} %pad_maximum_fusion), channel_id=1, source_target_pairs={{0,8},{8,16},{16,24},{24,32},{32,40},{40,48},{48,56},{56,64},{64,7... | collective-permute-start | bytes 294920 | tf_op jit(solution)/shard_map/ppermute | solution.py:16
  100.3 0.0 collective-permute-done.3
  100.3 0.0 collective-permute-done.4
  100.3 0.0 collective-permute-done.5
  100.4 0.0 collective-permute-done.6
  100.4 12.6 %collective-permute-done.7 = bf16[2,192,1,128]{3,1,2,0:T(8,128)(2,1)S(1)} collective-permute-done((bf16[2,192,1,128]{3,1,2,0:T(8,128)(2,1)S(1)}, bf16[2,192,1,128]{3,1,2,0:T(8,128)(2,1)S(1)}, u32[]{:S(2)}, u32[]{:S(2)}) %collective-permute-start.7) | collective-permute-done | bytes 98336 | tf_op jit(solution)/shard_map/ppermute | solution.py:16
  113.0 0.8 constant_dynamic-update-slice_fusion
  113.8 0.1 slice_bitcast_fusion.1
  113.9 0.0 copy-done
  113.9 0.0 copy-done.2
  113.9 0.0 copy-done.3
  113.9 2.3 %fusion.1 = (f32[4,192]{1,0:T(4,128)S(1)}, f32[1732,192,4]{0,1,2:T(8,128)S(1)}) fusion(f32[4,1732]{1,0:T(4,128)S(1)} %broadcast_select_fusion, s32[192,1732]{1,0:T(8,128)S(1)} %broadcast_subtract_fusion, s32[4]{0:T(128)S(1)} %copy-done.3, pred[4,1732]{1,0:T(4,128)(4,1)S(1)} %get-tuple-element.8, pred[4,1732]{1,0:T(4,128)(4,1)S(1)} %get-tuple-element.7, ...), kind=kOutput, calls=%fused_computation.6 | convolution fusion | flops 352052480 | bytes 7669812 | tf_op jit(solution)/shard_map/tkgd,skd->kgts/dot_general | solution.py:53
  116.2 3.5 %fusion.4 = f32[4,192]{1,0:T(4,128)S(1)} fusion(f32[4,192]{1,0:T(4,128)S(1)} %get-tuple-element.11, f32[4,1732]{1,0:T(4,128)S(1)} %broadcast_select_fusion, f32[1732,192,4]{0,1,2:T(8,128)S(1)} %get-tuple-element.12, pred[4,1732]{1,0:T(4,128)(4,1)S(1)} %get-tuple-element.8, s32[4]{0:T(128)S(1)} %copy-done.3, s32[192,1732]{1,0:T(8,128)S(1)} %broadcast_subtract_fusion, ...), kind=kLoop, calls=%fused_computation.9 | loop fusion | flops 13300992 | bytes 7032884 | tf_op jit(solution)/shard_map/reduce_sum | solution.py:72
  119.7 0.0 copy-start.1
  119.7 2.8 %fusion.8 = bf16[192,1,4,128]{3,0,2,1:T(8,128)(2,1)S(1)} fusion(f32[4,192]{1,0:T(4,128)S(1)} %fusion.4, f32[4,192]{1,0:T(4,128)S(1)} %get-tuple-element.11, f32[4,1732]{1,0:T(4,128)S(1)} %broadcast_select_fusion, f32[1732,192,4]{0,1,2:T(8,128)S(1)} %get-tuple-element.12, pred[4,1732]{1,0:T(4,128)(4,1)S(1)} %get-tuple-element.8, s32[4]{0:T(128)S(1)} %copy-done.3, ...), kind=kOutput, calls=%fused_computation.11 | convolution fusion | flops 356142080 | bytes 7672884 | tf_op jit(solution)/shard_map/kgts,skd->tkgd/dot_general | solution.py:73
  122.6 0.2 copy.12
  122.7 0.0 copy-done.1
  122.7 1.0 convolution_convert_fusion
  123.8 43.5 %all_to_all.5 = bf16[8,24,4096]{2,1,0:T(8,128)(2,1)S(1)} all-to-all(bf16[8,24,4096]{2,1,0:T(8,128)(2,1)S(1)} %bitcast.61), channel_id=1, replica_groups=mesh['seq_0'=2,'seq_1'=4,'seq_2'=8,'head'=8] {'head'}, dimensions={0} | all-to-all | bytes 3145728 | tf_op jit(solution)/shard_map/all_to_all | solution.py:38
  167.3 0.9 reduce_sum.61
  (15 shorter events, 0.2 us)
Async XLA Ops:
  0.0 113.9 %copy-start = (bf16[192,4,128]{2,1,0:T(4,128)(2,1)S(1)}, bf16[192,4,128]{2,1,0:T(4,128)(2,1)}, u32[]{:S(2)}) copy-start(bf16[192,4,128]{2,1,0:T(4,128)(2,1)} %param.7) | copy-start | bytes 589828
  0.0 113.9 %copy-start.2 = (pred[1732]{0:T(1024)(128)(4,1)S(1)}, pred[1732]{0:T(1024)(128)(4,1)}, u32[]{:S(2)}) copy-start(pred[1732]{0:T(1024)(128)(4,1)} %constant.40.clone.1) | copy-start | bytes 5200
  0.0 113.9 %copy-start.3 = (s32[4]{0:T(128)S(1)}, s32[4]{0:T(128)}, u32[]{:S(2)}) copy-start(s32[4]{0:T(128)} %param.10) | copy-start | bytes 52
  0.9 99.5 %collective-permute-start.6 = (bf16[2,192,1,128]{3,1,2,0:T(8,128)(2,1)S(1)}, bf16[2,192,1,128]{3,1,2,0:T(8,128)(2,1)S(1)}, u32[]{:S(2)}, u32[]{:S(2)}) collective-permute-start(bf16[2,192,1,128]{3,1,2,0:T(8,128)(2,1)S(1)} %pad_maximum_fusion), channel_id=1, source_target_pairs={{0,16},{8,24},{16,32},{24,40},{32,48},{40,56},{48,64},{56,72},{64,... | collective-permute-start | bytes 294920 | tf_op jit(solution)/shard_map/ppermute | solution.py:16
  5.4 94.9 %collective-permute-start.5 = (bf16[2,192,1,128]{3,1,2,0:T(8,128)(2,1)S(1)}, bf16[2,192,1,128]{3,1,2,0:T(8,128)(2,1)S(1)}, u32[]{:S(2)}, u32[]{:S(2)}) collective-permute-start(bf16[2,192,1,128]{3,1,2,0:T(8,128)(2,1)S(1)} %pad_maximum_fusion), channel_id=1, source_target_pairs={{0,24},{8,32},{16,40},{24,48},{32,56},{40,64},{48,72},{56,80},{64,... | collective-permute-start | bytes 294920 | tf_op jit(solution)/shard_map/ppermute | solution.py:16
  11.2 89.1 %collective-permute-start.4 = (bf16[2,192,1,128]{3,1,2,0:T(8,128)(2,1)S(1)}, bf16[2,192,1,128]{3,1,2,0:T(8,128)(2,1)S(1)}, u32[]{:S(2)}, u32[]{:S(2)}) collective-permute-start(bf16[2,192,1,128]{3,1,2,0:T(8,128)(2,1)S(1)} %pad_maximum_fusion), channel_id=1, source_target_pairs={{0,32},{8,40},{16,48},{24,56},{32,64},{40,72},{48,80},{56,88},{64,... | collective-permute-start | bytes 294920 | tf_op jit(solution)/shard_map/ppermute | solution.py:16
  15.1 85.2 %collective-permute-start.3 = (bf16[2,192,1,128]{3,1,2,0:T(8,128)(2,1)S(1)}, bf16[2,192,1,128]{3,1,2,0:T(8,128)(2,1)S(1)}, u32[]{:S(2)}, u32[]{:S(2)}) collective-permute-start(bf16[2,192,1,128]{3,1,2,0:T(8,128)(2,1)S(1)} %pad_maximum_fusion), channel_id=1, source_target_pairs={{0,40},{8,48},{16,56},{24,64},{32,72},{40,80},{48,88},{56,96},{64,... | collective-permute-start | bytes 294920 | tf_op jit(solution)/shard_map/ppermute | solution.py:16
  21.1 48.9 %collective-permute-start = (bf16[2,192,1,128]{3,1,2,0:T(8,128)(2,1)S(1)}, bf16[2,192,1,128]{3,1,2,0:T(8,128)(2,1)S(1)}, u32[]{:S(2)}, u32[]{:S(2)}) collective-permute-start(bf16[2,192,1,128]{3,1,2,0:T(8,128)(2,1)S(1)} %pad_maximum_fusion), channel_id=1, source_target_pairs={{0,64},{8,72},{16,80},{24,88},{32,96},{40,104},{48,112},{56,120},{... | collective-permute-start | bytes 294920 | tf_op jit(solution)/shard_map/ppermute | solution.py:16
  70.1 13.4 %collective-permute-start.1 = (bf16[2,192,1,128]{3,1,2,0:T(8,128)(2,1)S(1)}, bf16[2,192,1,128]{3,1,2,0:T(8,128)(2,1)S(1)}, u32[]{:S(2)}, u32[]{:S(2)}) collective-permute-start(bf16[2,192,1,128]{3,1,2,0:T(8,128)(2,1)S(1)} %pad_maximum_fusion), channel_id=1, source_target_pairs={{0,56},{8,64},{16,72},{24,80},{32,88},{40,96},{48,104},{56,112},{6... | collective-permute-start | bytes 294920 | tf_op jit(solution)/shard_map/ppermute | solution.py:16
  83.5 14.8 %collective-permute-start.2 = (bf16[2,192,1,128]{3,1,2,0:T(8,128)(2,1)S(1)}, bf16[2,192,1,128]{3,1,2,0:T(8,128)(2,1)S(1)}, u32[]{:S(2)}, u32[]{:S(2)}) collective-permute-start(bf16[2,192,1,128]{3,1,2,0:T(8,128)(2,1)S(1)} %pad_maximum_fusion), channel_id=1, source_target_pairs={{0,48},{8,56},{16,64},{24,72},{32,80},{40,88},{48,96},{56,104},{64... | collective-permute-start | bytes 294920 | tf_op jit(solution)/shard_map/ppermute | solution.py:16
  98.3 14.6 %collective-permute-start.7 = (bf16[2,192,1,128]{3,1,2,0:T(8,128)(2,1)S(1)}, bf16[2,192,1,128]{3,1,2,0:T(8,128)(2,1)S(1)}, u32[]{:S(2)}, u32[]{:S(2)}) collective-permute-start(bf16[2,192,1,128]{3,1,2,0:T(8,128)(2,1)S(1)} %pad_maximum_fusion), channel_id=1, source_target_pairs={{0,8},{8,16},{16,24},{24,32},{32,40},{40,48},{48,56},{56,64},{64,7... | collective-permute-start | bytes 294920 | tf_op jit(solution)/shard_map/ppermute | solution.py:16
  119.7 3.0 %copy-start.1 = (bf16[512,4096]{1,0:T(8,128)(2,1)S(1)}, bf16[512,4096]{1,0:T(8,128)(2,1)}, u32[]{:S(2)}) copy-start(bf16[512,4096]{1,0:T(8,128)(2,1)} %param.13) | copy-start | bytes 12582916
